TPU v7x, 32 devices: a whole 2x2x4 slice. The times are simulated.
32 devices in a mesh: win: 16 (over z, y, core), head: 2 (over x).
Axes of the slice: x: 2, y: 2, z: 4, core: 2. Of those that a mesh axis runs over, the one named last changes fastest.
Arguments:
- qkv: bfloat16 [3, 16, 96, 48, 1024], P(None, 'win', 'head'), may hold values from -10 to 10
Outputs:
- attended: bfloat16 [16, 96, 48, 1024], P('win', 'head')
All inputs are finite; a program needn't handle non-finite values.
Results may differ from a plain program's by a relative error of at most 0.0047.
Values may be sent and summed in bfloat16 or wider, within the bound.
A program may use at most 192 MiB of HBM per device.

v0:
```python
import math
import jax
import jax.numpy as jnp
from jax import lax
from jax.sharding import PartitionSpec as P

HEAD_DIM = 128


def from_behind(shard, axis, by):
    count = lax.axis_size(axis)
    return lax.ppermute(shard, axis, [(i, (i + by) % count) for i in range(count)])


def partner(value, axis, apart):
    mask = 2**apart
    pairs = [(source, source ^ mask) for source in range(lax.axis_size(axis))]
    return lax.ppermute(value, axis, pairs)


def attend(queries, keys, values, labels_query, labels_key):
    query_count, head_count, head_width = queries.shape
    block_rows = math.gcd(query_count, 576)
    score_scale = 1.0 / math.sqrt(head_width)

    def one_block(pieces):
        query_block, label_block = pieces
        scores = (
            jnp.einsum("qhd,khd->hqk", query_block, keys, preferred_element_type=jnp.float32)
            * score_scale
        )
        allowed = label_block[:, None] == labels_key[None, :]
        scores = jnp.where(allowed[None], scores, -jnp.inf)
        row_max = jnp.max(scores, axis=-1, keepdims=True)
        weights = jnp.exp(scores - row_max)
        row_total = jnp.sum(weights, axis=-1, keepdims=True)
        mixture = jnp.einsum(
            "hqk,khd->qhd", weights.astype(jnp.bfloat16), values, preferred_element_type=jnp.float32
        )
        return (mixture / jnp.transpose(row_total, (1, 0, 2))).astype(jnp.bfloat16)

    query_blocks = queries.reshape(query_count // block_rows, block_rows, head_count, head_width)
    label_blocks = labels_query.reshape(query_count // block_rows, block_rows)
    return lax.map(one_block, (query_blocks, label_blocks)).reshape(
        query_count, head_count, head_width
    )


def window_attention(window, labels):
    row_count, side_cells, channels = (window.shape[1], window.shape[2], window.shape[3])
    head_count = channels // HEAD_DIM
    window_parts = window.reshape(
        3, row_count // side_cells, side_cells * side_cells, head_count, HEAD_DIM
    )
    label_parts = labels.reshape(row_count // side_cells, side_cells * side_cells)
    outputs = []
    for window_row in range(row_count // side_cells):
        outputs.append(
            attend(
                window_parts[0, window_row],
                window_parts[1, window_row],
                window_parts[2, window_row],
                label_parts[window_row],
                label_parts[window_row],
            )
        )
    return jnp.stack(outputs).reshape(row_count, side_cells, channels)


def body(qkv):
    side_cells = qkv.shape[3]
    half_cols = side_cells // 2
    tokens = qkv[:, 0]
    arrived = from_behind(tokens[:, :, :half_cols], "win", -2)
    tokens = jnp.concatenate([tokens[:, :, half_cols:], arrived], axis=2)
    head_view = lax.all_to_all(tokens, "head", split_axis=3, concat_axis=1, tiled=True)
    half_rows = head_view.shape[1]
    crossing = partner(head_view[:, :half_cols], "win", 0)
    extended = jnp.concatenate([head_view[:, half_cols:], crossing], axis=1)
    lat_half = lax.axis_index("win") % 2
    row_index = jnp.arange(half_rows, dtype=jnp.int32)[:, None]
    wrapped = jnp.logical_and(lat_half == 1, row_index >= half_rows - half_cols)
    labels = jnp.broadcast_to(jnp.where(wrapped, 1, 0).astype(jnp.int32), (half_rows, side_cells))
    result = window_attention(extended, labels)
    returned = partner(result[half_rows - half_cols :], "win", 0)
    row_fixed = jnp.concatenate([returned, result[: half_rows - half_cols]], axis=0)
    restored = lax.all_to_all(row_fixed, "head", split_axis=0, concat_axis=2, tiled=True)
    from_west = from_behind(restored[:, half_cols:], "win", 2)
    restored = jnp.concatenate([from_west, restored[:, :half_cols]], axis=1)
    return restored[None]


def solution(mesh):
    in_specs = (P(None, "win", "head", None, None),)
    out_specs = P("win", "head", None, None)
    return jax.shard_map(body, mesh=mesh, in_specs=in_specs, out_specs=out_specs, check_vma=False)
```

profile of v0, /device:TPU:0, one launch (start us, length us, event | category | flops | bytes accessed | tf_op | source)
XLA Modules:
  0.0 1056.7 jit_solution(9154201426480805091)
XLA Ops:
  0.0 6.6 fusion.44
  6.6 6.1 collective-permute-start
  12.7 151.6 %collective-permute-done = bf16[3,48,24,1024]{3,2,1,0:T(8,128)(2,1)S(1)} collective-permute-done((bf16[3,48,24,1024]{3,2,1,0:T(8,128)(2,1)S(1)}, bf16[3,48,24,1024]{3,2,1,0:T(8,128)(2,1)S(1)}, u32[]{:S(2)}, u32[]{:S(2)}) %collective-permute-start) | collective-permute-done | bytes 7077920 | tf_op jit(solution)/shard_map/ppermute | solution.py:12
  164.3 6.7 pad_maximum_fusion
  171.0 42.0 %copy.38 = bf16[3,48,48,1024]{2,1,0,3:T(8,128)(2,1)} copy(bf16[3,48,48,1024]{3,2,1,0:T(8,128)(2,1)} %pad_maximum_fusion) | data formatting | bytes 28311552 | tf_op jit(solution)/shard_map/concatenate | solution.py:75
  213.1 66.4 %reshape.117 = bf16[2,2,1769472]{2,1,0:T(2,128)(2,1)} reshape(bf16[1024,3,48,48]{3,2,1,0:T(8,128)(2,1)} %bitcast.107) | data formatting | bytes 28311552
  279.5 169.9 %all_to_all.36 = bf16[2,2,1769472]{2,1,0:T(2,128)(2,1)} all-to-all(bf16[2,2,1769472]{2,1,0:T(2,128)(2,1)} %reshape.117), channel_id=1, replica_groups=mesh['win'=16,'head'=2] {'head'}, dimensions={0} | all-to-all | bytes 28311552 | tf_op jit(solution)/shard_map/all_to_all | solution.py:76
  449.4 57.7 %reshape.118 = bf16[1024,3,48,48]{3,2,1,0:T(8,128)(2,1)} reshape(bf16[2,2,1769472]{2,1,0:T(2,128)(2,1)} %all_to_all.36) | data formatting | bytes 28311552
  507.1 59.6 %copy.52 = bf16[3,48,48,2,512]{4,3,2,1,0:T(2,128)(2,1)} copy(bf16[3,48,48,2,512]{2,1,0,4,3:T(8,128)(2,1)} %bitcast.108) | data formatting | bytes 28311552 | tf_op jit(solution)/shard_map/all_to_all | solution.py:76
  566.7 9.2 copy.40
  576.0 5.0 copy-done
  581.0 2.0 slice.95
  585.8 1.3 broadcast_in_dim.76
  587.1 1.3 broadcast_in_dim.77
  588.4 1.4 broadcast_in_dim.78
  589.9 5.5 slice.94
  595.4 8.2 pad_maximum_fusion.1
  603.6 20.3 %reshape.99 = bf16[3,2,2304,4,128]{4,3,2,1,0:T(4,128)(2,1)} reshape(bf16[3,96,48,512]{3,2,1,0:T(8,128)(2,1)} %pad_maximum_fusion.1) | data formatting | bytes 28311552 | tf_op jit(solution)/shard_map/reshape | solution.py:52
  623.9 11.5 %slice_bitcast_fusion.2 = (bf16[2304,4,128]{2,1,0:T(4,128)(2,1)S(1)}, bf16[2304,4,128]{2,1,0:T(4,128)(2,1)}, bf16[2304,4,128]{2,1,0:T(4,128)(2,1)}, bf16[1,1,230...) fusion(bf16[3,2,2304,4,128]{4,3,2,1,0:T(4,128)(2,1)} %reshape.99), kind=kLoop, calls=%fused_computation.45 | loop fusion | bytes 28311552 | tf_op jit(solution)/shard_map/squeeze | solution.py:62
  635.7 1.8 copy.43
  637.5 1.9 broadcast.86.clone2.1
  639.4 131.7 %while.22 = (s32[]{:T(128)}, bf16[4,576,4,128]{3,1,0,2:T(8,128)(2,1)}, s32[4,576]{1,0:T(4,128)S(1)}, bf16[4,576,4,128]{3,2,1,0:T(4,128)(2,1)}, bf16[2304,4,128]{...) while((s32[]{:T(128)}, ...), condition=%wide.region_3.4_spmd.clone, body=%wide.region_0.3_spmd.clone.sunk | while | flops 2778213888 | bytes 85615160 | solution.py:44
  640.4 1.3 constant_dynamic-slice_fusion.4
  641.7 9.5 fusion.65
  651.2 10.6 %fusion.66 = f32[4,576]{1,0:T(4,128)S(1)} fusion(f32[4,576,2304]{2,1,0:T(8,128)} %get-tuple-element.309, f32[4,576]{1,0:T(4,128)S(1)} %get-tuple-element.310, pred[576,2304]{1,0:T(8,128)(4,1)S(1)} %broadcast_compare_fusion.4), kind=kLoop, calls=%fused_computation.5.clone.1 | loop fusion | flops 21231360 | bytes 22579200 | tf_op jit(solution)/shard_map/while/body/eval_jaxpr/reduce_sum | solution.py:36
  661.9 10.5 fusion.67
  673.3 1.3 constant_dynamic-slice_fusion.4
  674.6 9.5 fusion.65
  684.2 10.6 %fusion.66 = f32[4,576]{1,0:T(4,128)S(1)} fusion(f32[4,576,2304]{2,1,0:T(8,128)} %get-tuple-element.309, f32[4,576]{1,0:T(4,128)S(1)} %get-tuple-element.310, pred[576,2304]{1,0:T(8,128)(4,1)S(1)} %broadcast_compare_fusion.4), kind=kLoop, calls=%fused_computation.5.clone.1 | loop fusion | flops 21231360 | bytes 22579200 | tf_op jit(solution)/shard_map/while/body/eval_jaxpr/reduce_sum | solution.py:36
  694.8 10.5 fusion.67
  707.5 9.5 fusion.65
  717.1 10.6 %fusion.66 = f32[4,576]{1,0:T(4,128)S(1)} fusion(f32[4,576,2304]{2,1,0:T(8,128)} %get-tuple-element.309, f32[4,576]{1,0:T(4,128)S(1)} %get-tuple-element.310, pred[576,2304]{1,0:T(8,128)(4,1)S(1)} %broadcast_compare_fusion.4), kind=kLoop, calls=%fused_computation.5.clone.1 | loop fusion | flops 21231360 | bytes 22579200 | tf_op jit(solution)/shard_map/while/body/eval_jaxpr/reduce_sum | solution.py:36
  727.7 10.5 fusion.67
  740.5 9.5 fusion.65
  750.0 10.6 %fusion.66 = f32[4,576]{1,0:T(4,128)S(1)} fusion(f32[4,576,2304]{2,1,0:T(8,128)} %get-tuple-element.309, f32[4,576]{1,0:T(4,128)S(1)} %get-tuple-element.310, pred[576,2304]{1,0:T(8,128)(4,1)S(1)} %broadcast_compare_fusion.4), kind=kLoop, calls=%fused_computation.5.clone.1 | loop fusion | flops 21231360 | bytes 22579200 | tf_op jit(solution)/shard_map/while/body/eval_jaxpr/reduce_sum | solution.py:36
  760.7 10.5 fusion.67
  771.1 2.1 copy.47
  773.5 1.8 copy.48
  775.3 1.9 broadcast.86.clone2
  777.1 134.7 %while.23 = (s32[]{:T(128)}, bf16[4,576,4,128]{3,1,0,2:T(8,128)(2,1)}, s32[4,576]{1,0:T(4,128)}, bf16[4,576,4,128]{3,2,1,0:T(4,128)(2,1)}, bf16[2304,4,128]{2,0,...) while((s32[]{:T(128)}, bf16[4,576,4,128]{3,1,0,2:T(8,128)(2,1)}, ...), condition=%wide.region_7.8_spmd.clone, body=%wide.region_4.7_spmd.clone.sunk | while | flops 2778213888 | bytes 85615160 | solution.py:44
  779.1 1.3 constant_dynamic-slice_fusion.5
  780.4 9.5 fusion.71
  789.9 10.6 %fusion.72 = f32[4,576]{1,0:T(4,128)S(1)} fusion(f32[4,576,2304]{2,1,0:T(8,128)} %get-tuple-element.318, f32[4,576]{1,0:T(4,128)S(1)} %get-tuple-element.319, pred[576,2304]{1,0:T(8,128)(4,1)S(1)} %broadcast_compare_fusion.5), kind=kLoop, calls=%fused_computation.23.clone.1 | loop fusion | flops 21231360 | bytes 22579200 | tf_op jit(solution)/shard_map/while/body/eval_jaxpr/reduce_sum | solution.py:36
  800.6 10.4 fusion.73
  812.7 1.3 constant_dynamic-slice_fusion.5
  814.0 9.5 fusion.71
  823.5 10.6 %fusion.72 = f32[4,576]{1,0:T(4,128)S(1)} fusion(f32[4,576,2304]{2,1,0:T(8,128)} %get-tuple-element.318, f32[4,576]{1,0:T(4,128)S(1)} %get-tuple-element.319, pred[576,2304]{1,0:T(8,128)(4,1)S(1)} %broadcast_compare_fusion.5), kind=kLoop, calls=%fused_computation.23.clone.1 | loop fusion | flops 21231360 | bytes 22579200 | tf_op jit(solution)/shard_map/while/body/eval_jaxpr/reduce_sum | solution.py:36
  834.2 10.4 fusion.73
  846.3 1.3 constant_dynamic-slice_fusion.5
  847.6 9.5 fusion.71
  857.1 10.6 %fusion.72 = f32[4,576]{1,0:T(4,128)S(1)} fusion(f32[4,576,2304]{2,1,0:T(8,128)} %get-tuple-element.318, f32[4,576]{1,0:T(4,128)S(1)} %get-tuple-element.319, pred[576,2304]{1,0:T(8,128)(4,1)S(1)} %broadcast_compare_fusion.5), kind=kLoop, calls=%fused_computation.23.clone.1 | loop fusion | flops 21231360 | bytes 22579200 | tf_op jit(solution)/shard_map/while/body/eval_jaxpr/reduce_sum | solution.py:36
  867.8 10.4 fusion.73
  879.9 1.3 constant_dynamic-slice_fusion.5
  881.2 9.5 fusion.71
  890.8 10.6 %fusion.72 = f32[4,576]{1,0:T(4,128)S(1)} fusion(f32[4,576,2304]{2,1,0:T(8,128)} %get-tuple-element.318, f32[4,576]{1,0:T(4,128)S(1)} %get-tuple-element.319, pred[576,2304]{1,0:T(8,128)(4,1)S(1)} %broadcast_compare_fusion.5), kind=kLoop, calls=%fused_computation.23.clone.1 | loop fusion | flops 21231360 | bytes 22579200 | tf_op jit(solution)/shard_map/while/body/eval_jaxpr/reduce_sum | solution.py:36
  901.4 10.4 fusion.73
  911.9 2.8 pad_maximum_fusion.2
  914.7 12.0 %copy.50 = bf16[2,2304,4,128]{3,2,1,0:T(4,128)(2,1)} copy(bf16[2,2304,4,128]{3,1,2,0:T(8,128)(2,1)S(1)} %pad_maximum_fusion.2) | data formatting | bytes 9437184 | tf_op jit(solution)/shard_map/stack | solution.py:67
  926.7 8.0 reshape.100
  934.7 1.5 slice.102
  936.8 2.5 collective-permute-done.2
  939.7 56.5 %all_to_all.37 = bf16[96,48,512]{2,1,0:T(8,128)(2,1)S(1)} all-to-all(bf16[96,48,512]{2,1,0:T(8,128)(2,1)S(1)} %pad_maximum_fusion.3), channel_id=1, replica_groups=mesh['win'=16,'head'=2] {'head'}, dimensions={0} | all-to-all | bytes 9437184 | tf_op jit(solution)/shard_map/all_to_all | solution.py:87
  997.7 55.8 %collective-permute-done.3 = bf16[48,24,1024]{2,1,0:T(8,128)(2,1)S(1)} collective-permute-done((bf16[48,24,1024]{2,1,0:T(8,128)(2,1)S(1)}, bf16[48,24,1024]{2,1,0:T(8,128)(2,1)S(1)}, u32[]{:S(2)}, u32[]{:S(2)}) %collective-permute-start.3) | collective-permute-done | bytes 2359328 | tf_op jit(solution)/shard_map/ppermute | solution.py:12
  1053.5 2.7 maximum_bitcast_fusion
  (70 shorter events, 19.0 us)
Async XLA Ops:
  6.6 157.7 %collective-permute-start = (bf16[3,48,24,1024]{3,2,1,0:T(8,128)(2,1)S(1)}, bf16[3,48,24,1024]{3,2,1,0:T(8,128)(2,1)S(1)}, u32[]{:S(2)}, u32[]{:S(2)}) collective-permute-start(bf16[3,48,24,1024]{3,2,1,0:T(8,128)(2,1)S(1)} %get-tuple-element.219), channel_id=1, source_target_pairs={{0,28},{2,30},{4,0},{6,2},{8,4},{10,6},{12,8},{14,10},{16,12},{18,... | collective-permute-start | bytes 21233672 | tf_op jit(solution)/shard_map/ppermute | solution.py:12
  576.0 5.1 copy-start
  583.0 12.4 %collective-permute-start.1 = (bf16[3,24,48,512]{3,2,1,0:T(8,128)(2,1)}, bf16[3,24,48,512]{3,2,1,0:T(8,128)(2,1)S(1)}, u32[]{:S(2)}, u32[]{:S(2)}) collective-permute-start(bf16[3,24,48,512]{3,2,1,0:T(8,128)(2,1)} %slice.95), channel_id=1, source_target_pairs={{0,2},{2,0},{4,6},{6,4},{8,10},{10,8},{12,14},{14,12},{16,18},{18,... | collective-permute-start | bytes 10616840 | tf_op jit(solution)/shard_map/ppermute | solution.py:18
  651.2 10.7 %copy-start.3 = (bf16[2304,4,128]{2,0,1:T(8,128)(2,1)S(1)}, bf16[2304,4,128]{2,0,1:T(8,128)(2,1)}, u32[]{:S(2)}) copy-start(bf16[2304,4,128]{2,0,1:T(8,128)(2,1)} %get-tuple-element.365) | copy-start | bytes 7077892 | tf_op jit(solution)/shard_map/while
  684.1 10.7 %copy-start.3 = (bf16[2304,4,128]{2,0,1:T(8,128)(2,1)S(1)}, bf16[2304,4,128]{2,0,1:T(8,128)(2,1)}, u32[]{:S(2)}) copy-start(bf16[2304,4,128]{2,0,1:T(8,128)(2,1)} %get-tuple-element.365) | copy-start | bytes 7077892 | tf_op jit(solution)/shard_map/while
  717.1 10.7 %copy-start.3 = (bf16[2304,4,128]{2,0,1:T(8,128)(2,1)S(1)}, bf16[2304,4,128]{2,0,1:T(8,128)(2,1)}, u32[]{:S(2)}) copy-start(bf16[2304,4,128]{2,0,1:T(8,128)(2,1)} %get-tuple-element.365) | copy-start | bytes 7077892 | tf_op jit(solution)/shard_map/while
  750.0 10.7 %copy-start.3 = (bf16[2304,4,128]{2,0,1:T(8,128)(2,1)S(1)}, bf16[2304,4,128]{2,0,1:T(8,128)(2,1)}, u32[]{:S(2)}) copy-start(bf16[2304,4,128]{2,0,1:T(8,128)(2,1)} %get-tuple-element.365) | copy-start | bytes 7077892 | tf_op jit(solution)/shard_map/while
  771.1 2.4 copy-start.1
  773.2 3.9 copy-start.4
  789.9 10.7 %copy-start.2 = (bf16[2304,4,128]{2,0,1:T(8,128)(2,1)S(1)}, bf16[2304,4,128]{2,0,1:T(8,128)(2,1)}, u32[]{:S(2)}) copy-start(bf16[2304,4,128]{2,0,1:T(8,128)(2,1)} %get-tuple-element.341) | copy-start | bytes 7077892 | tf_op jit(solution)/shard_map/while
  823.5 10.7 %copy-start.2 = (bf16[2304,4,128]{2,0,1:T(8,128)(2,1)S(1)}, bf16[2304,4,128]{2,0,1:T(8,128)(2,1)}, u32[]{:S(2)}) copy-start(bf16[2304,4,128]{2,0,1:T(8,128)(2,1)} %get-tuple-element.341) | copy-start | bytes 7077892 | tf_op jit(solution)/shard_map/while
  857.1 10.7 %copy-start.2 = (bf16[2304,4,128]{2,0,1:T(8,128)(2,1)S(1)}, bf16[2304,4,128]{2,0,1:T(8,128)(2,1)}, u32[]{:S(2)}) copy-start(bf16[2304,4,128]{2,0,1:T(8,128)(2,1)} %get-tuple-element.341) | copy-start | bytes 7077892 | tf_op jit(solution)/shard_map/while
  890.8 10.7 %copy-start.2 = (bf16[2304,4,128]{2,0,1:T(8,128)(2,1)S(1)}, bf16[2304,4,128]{2,0,1:T(8,128)(2,1)}, u32[]{:S(2)}) copy-start(bf16[2304,4,128]{2,0,1:T(8,128)(2,1)} %get-tuple-element.341) | copy-start | bytes 7077892 | tf_op jit(solution)/shard_map/while
  934.7 4.6 slice-start
  936.2 3.0 collective-permute-start.2
  997.3 56.2 %collective-permute-start.3 = (bf16[48,24,1024]{2,1,0:T(8,128)(2,1)S(1)}, bf16[48,24,1024]{2,1,0:T(8,128)(2,1)S(1)}, u32[]{:S(2)}, u32[]{:S(2)}) collective-permute-start(bf16[48,24,1024]{2,1,0:T(8,128)(2,1)S(1)} %get-tuple-element.220), channel_id=1, source_target_pairs={{0,4},{2,6},{4,8},{6,10},{8,12},{10,14},{12,16},{14,18},{16,20},{1... | collective-permute-start | bytes 7077896 | tf_op jit(solution)/shard_map/ppermute | solution.py:12
where the time goes:
time: 1070 us; the launch traced here: 1060 us
  local copies, waits for them, and re-layouts  340 us (32%)
  blocking collectives  226 us (21%)
  waiting for transfers between devices  210 us (20%)
  matrix products  160 us (15%)
  other arithmetic  112 us (10%)
    ppermute x2, waiting for transfers between devices, from_behind(): lax.ppermute(shard, axis, [(i, (i + by) % count) for i in range(count)])  207 us
    all_to_all x1, blocking collectives, body(): lax.all_to_all(tokens, 'head', split_axis=3, concat_axis=1, tiled=True)  170 us
    unnamed x12, local copies, waits for them, and re-layouts  135 us
    reduce_sum x8, other arithmetic, one_block(): row_total = jnp.sum(weights, axis=-1, keepdims=True)  85.1 us
    dot_general x8, matrix products, one_block(): jnp.einsum('hqk,khd->qhd', weights.astype(jnp.bfloat16), values, preferre...  83.6 us
    dot_general x8, matrix products, one_block(): jnp.einsum('qhd,khd->hqk', query_block, keys, preferred_element_type=jnp....  76.4 us
    all_to_all x2, local copies, waits for them, and re-layouts, body(): lax.all_to_all(tokens, 'head', split_axis=3, concat_axis=1, tiled=True)  68.8 us
    all_to_all x1, blocking collectives, body(): lax.all_to_all(row_fixed, 'head', split_axis=0, concat_axis=2, tiled=True)  56.5 us
  transfers between devices with their start and end apart: 4, of which 3 were waited for; matrix products, arithmetic and copies ran while one was open for 1% of the time, Pallas kernels for 0%

commit v1 on v0

--- a/solution.py
+++ b/solution.py
@@ -73,7 +73,10 @@
     tokens = qkv[:, 0]
     arrived = from_behind(tokens[:, :, :half_cols], "win", -2)
     tokens = jnp.concatenate([tokens[:, :, half_cols:], arrived], axis=2)
-    head_view = lax.all_to_all(tokens, "head", split_axis=3, concat_axis=1, tiled=True)
+    head_view = jnp.concatenate(
+        lax.all_to_all(jnp.stack(jnp.split(tokens, lax.axis_size("head"), axis=3)), "head", 0, 0),
+        axis=1,
+    )
     half_rows = head_view.shape[1]
     crossing = partner(head_view[:, :half_cols], "win", 0)
     extended = jnp.concatenate([head_view[:, half_cols:], crossing], axis=1)

time: 1070 us -> 809 us (0.76); the launches traced: 1060 us -> 807 us
  local copies, waits for them, and re-layouts: 340 us -> 107 us
  blocking collectives: 226 us -> 214 us
    unnamed x12 -> x10, local copies, waits for them, and re-layouts: 135 us -> 11.3 us
    all_to_all x2 -> x1, local copies, waits for them, and re-layouts: 68.8 us -> 2.47 us  [body(): lax.all_to_all(jnp.stack(jnp.split(tokens, lax.axis_size('head'), axis=3)...]
    concatenate x1 -> x0, local copies, waits for them, and re-layouts: 42 us -> none  [body(): tokens = jnp.concatenate([tokens[:, :, half_cols:], arrived], axis=2)]
    all_to_all x1, blocking collectives: 170 us -> 157 us  [body(): lax.all_to_all(jnp.stack(jnp.split(tokens, lax.axis_size('head'), axis=3)...]
  transfers between devices with their start and end apart: 4 -> 4, of which waited for: 3 -> 3; matrix products, arithmetic and copies ran while one was open for 1% -> 2% of each run, Pallas kernels for 0% -> 0%
where the time goes in v1:
time: 809 us; the launch traced here: 807 us
  blocking collectives  214 us (26%)
  waiting for transfers between devices  210 us (26%)
  matrix products  160 us (20%)
  other arithmetic  109 us (13%)
  local copies, waits for them, and re-layouts  107 us (13%)
    ppermute x2, waiting for transfers between devices, from_behind(): lax.ppermute(shard, axis, [(i, (i + by) % count) for i in range(count)])  207 us
    all_to_all x1, blocking collectives, body(): lax.all_to_all(jnp.stack(jnp.split(tokens, lax.axis_size('head'), axis=3)...  157 us
    reduce_sum x8, other arithmetic, one_block(): row_total = jnp.sum(weights, axis=-1, keepdims=True)  85.1 us
    dot_general x8, matrix products, one_block(): jnp.einsum('hqk,khd->qhd', weights.astype(jnp.bfloat16), values, preferre...  83.6 us
    dot_general x8, matrix products, one_block(): jnp.einsum('qhd,khd->hqk', query_block, keys, preferred_element_type=jnp....  76.4 us
    all_to_all x1, blocking collectives, body(): lax.all_to_all(row_fixed, 'head', split_axis=0, concat_axis=2, tiled=True)  56.5 us
    reshape x1, local copies, waits for them, and re-layouts, window_attention(): window.reshape(3, row_count // side_cells, side_cells * side_cells, head_...  20.3 us
  transfers between devices with their start and end apart: 4, of which 3 were waited for; matrix products, arithmetic and copies ran while one was open for 2% of the time, Pallas kernels for 0%

profile of v1, /device:TPU:0, one launch (start us, length us, event | category | flops | bytes accessed | tf_op | source)
XLA Modules:
  0.0 806.7 jit_solution(11438084062621293780)
XLA Ops:
  0.0 6.1 fusion.47
  6.1 6.1 collective-permute-start
  12.2 151.6 %collective-permute-done = bf16[3,48,24,1024]{3,2,1,0:T(8,128)(2,1)S(1)} collective-permute-done((bf16[3,48,24,1024]{3,2,1,0:T(8,128)(2,1)S(1)}, bf16[3,48,24,1024]{3,2,1,0:T(8,128)(2,1)S(1)}, u32[]{:S(2)}, u32[]{:S(2)}) %collective-permute-start) | collective-permute-done | bytes 7077920 | tf_op jit(solution)/shard_map/ppermute | solution.py:12
  163.8 1.9 fusion.45
  165.7 1.6 pad_maximum_fusion
  167.3 157.1 %all_to_all.23 = bf16[2,3,48,48,512]{4,3,2,1,0:T(8,128)(2,1)S(1)} all-to-all(bf16[2,3,48,48,512]{4,3,2,1,0:T(8,128)(2,1)S(1)} %pad_maximum_fusion), channel_id=1, replica_groups=mesh['win'=16,'head'=2] {'head'}, dimensions={0} | all-to-all | bytes 28311552 | tf_op jit(solution)/shard_map/all_to_all | solution.py:77
  324.4 2.5 copy.25
  326.8 5.0 copy-done
  331.9 2.0 slice.95
  333.9 1.1 slice_bitcast_fusion.5
  336.7 1.3 broadcast_in_dim.76
  338.0 1.3 broadcast_in_dim.77
  339.3 1.4 broadcast_in_dim.78
  340.8 5.5 slice.94
  346.3 8.2 %pad_maximum_fusion.1 = bf16[3,96,48,512]{3,2,1,0:T(8,128)(2,1)} fusion(bf16[3,24,48,512]{3,2,1,0:T(8,128)(2,1)S(1)} %collective-permute-done.1, bf16[3,72,48,512]{3,2,1,0:T(8,128)(2,1)S(1)} %slice.94), kind=kLoop, calls=%fused_computation.41 | loop fusion | flops 7077888 | bytes 28311552 | tf_op jit(solution)/shard_map/concatenate | solution.py:82
  354.5 20.3 %reshape.107 = bf16[3,2,2304,4,128]{4,3,2,1,0:T(4,128)(2,1)} reshape(bf16[3,96,48,512]{3,2,1,0:T(8,128)(2,1)} %pad_maximum_fusion.1) | data formatting | bytes 28311552 | tf_op jit(solution)/shard_map/reshape | solution.py:52
  374.8 11.3 %slice_bitcast_fusion.2 = (bf16[2304,4,128]{2,1,0:T(4,128)(2,1)S(1)}, bf16[2304,4,128]{2,1,0:T(4,128)(2,1)}, bf16[2304,4,128]{2,1,0:T(4,128)(2,1)}, bf16[1,1,230...) fusion(bf16[3,2,2304,4,128]{4,3,2,1,0:T(4,128)(2,1)} %reshape.107), kind=kLoop, calls=%fused_computation.51 | loop fusion | bytes 28311552 | tf_op jit(solution)/shard_map/squeeze | solution.py:62
  386.4 1.8 copy.28
  388.2 1.9 broadcast.86.clone2.1
  390.1 131.7 %while.22 = (s32[]{:T(128)}, bf16[4,576,4,128]{3,1,0,2:T(8,128)(2,1)}, s32[4,576]{1,0:T(4,128)S(1)}, bf16[4,576,4,128]{3,2,1,0:T(4,128)(2,1)}, bf16[2304,4,128]{...) while((s32[]{:T(128)}, ...), condition=%wide.region_3.4_spmd.clone, body=%wide.region_0.3_spmd.clone.sunk | while | flops 2778213888 | bytes 85615160 | solution.py:44
  391.1 1.3 constant_dynamic-slice_fusion.4
  392.4 9.5 %fusion.68 = (f32[4,576]{1,0:T(4,128)S(1)}, f32[4,576,2304]{2,1,0:T(8,128)}) fusion(pred[576,2304]{1,0:T(8,128)(4,1)S(1)} %broadcast_compare_fusion.4, bf16[2304,4,128]{2,0,1:T(8,128)(2,1)S(1)} %get-tuple-element.352, bf16[1,576,4,128]{3,2,1,0:T(4,128)(2,1)S(1)} %constant_dynamic-slice_fusion.4), kind=kOutput, calls=%fused_computation.4.clone.1 | convolution fusion | flops 1374877440 | bytes 25519104 | tf_op jit(solution)/shard_map/while/body/eval_jaxpr/qhd,khd->hqk/dot_general | solution.py:29
  401.9 10.6 %fusion.69 = f32[4,576]{1,0:T(4,128)S(1)} fusion(f32[4,576,2304]{2,1,0:T(8,128)} %get-tuple-element.297, f32[4,576]{1,0:T(4,128)S(1)} %get-tuple-element.298, pred[576,2304]{1,0:T(8,128)(4,1)S(1)} %broadcast_compare_fusion.4), kind=kLoop, calls=%fused_computation.5.clone.1 | loop fusion | flops 21231360 | bytes 22579200 | tf_op jit(solution)/shard_map/while/body/eval_jaxpr/reduce_sum | solution.py:36
  412.6 10.4 %fusion.70 = bf16[4,576,4,128]{3,1,0,2:T(8,128)(2,1)} fusion(bf16[4,576,4,128]{3,1,0,2:T(8,128)(2,1)} %get-tuple-element.341, s32[]{:T(128)} %get-tuple-element.340, bf16[2304,4,128]{2,0,1:T(8,128)(2,1)S(1)} %copy-done.3, f32[4,576,2304]{2,1,0:T(8,128)} %get-tuple-element.297, f32[4,576]{1,0:T(4,128)S(1)} %get-tuple-element.298, ...), kind=kOutput, calls=%fused_computation.13.clone.1 | convolution fusion | flops 1380777984 | bytes 25528832 | tf_op jit(solution)/shard_map/while/body/eval_jaxpr/hqk,khd->qhd/dot_general | solution.py:37
  424.0 1.3 constant_dynamic-slice_fusion.4
  425.3 9.5 %fusion.68 = (f32[4,576]{1,0:T(4,128)S(1)}, f32[4,576,2304]{2,1,0:T(8,128)}) fusion(pred[576,2304]{1,0:T(8,128)(4,1)S(1)} %broadcast_compare_fusion.4, bf16[2304,4,128]{2,0,1:T(8,128)(2,1)S(1)} %get-tuple-element.352, bf16[1,576,4,128]{3,2,1,0:T(4,128)(2,1)S(1)} %constant_dynamic-slice_fusion.4), kind=kOutput, calls=%fused_computation.4.clone.1 | convolution fusion | flops 1374877440 | bytes 25519104 | tf_op jit(solution)/shard_map/while/body/eval_jaxpr/qhd,khd->hqk/dot_general | solution.py:29
  434.8 10.6 %fusion.69 = f32[4,576]{1,0:T(4,128)S(1)} fusion(f32[4,576,2304]{2,1,0:T(8,128)} %get-tuple-element.297, f32[4,576]{1,0:T(4,128)S(1)} %get-tuple-element.298, pred[576,2304]{1,0:T(8,128)(4,1)S(1)} %broadcast_compare_fusion.4), kind=kLoop, calls=%fused_computation.5.clone.1 | loop fusion | flops 21231360 | bytes 22579200 | tf_op jit(solution)/shard_map/while/body/eval_jaxpr/reduce_sum | solution.py:36
  445.5 10.5 %fusion.70 = bf16[4,576,4,128]{3,1,0,2:T(8,128)(2,1)} fusion(bf16[4,576,4,128]{3,1,0,2:T(8,128)(2,1)} %get-tuple-element.341, s32[]{:T(128)} %get-tuple-element.340, bf16[2304,4,128]{2,0,1:T(8,128)(2,1)S(1)} %copy-done.3, f32[4,576,2304]{2,1,0:T(8,128)} %get-tuple-element.297, f32[4,576]{1,0:T(4,128)S(1)} %get-tuple-element.298, ...), kind=kOutput, calls=%fused_computation.13.clone.1 | convolution fusion | flops 1380777984 | bytes 25528832 | tf_op jit(solution)/shard_map/while/body/eval_jaxpr/hqk,khd->qhd/dot_general | solution.py:37
  457.0 1.3 constant_dynamic-slice_fusion.4
  458.2 9.5 %fusion.68 = (f32[4,576]{1,0:T(4,128)S(1)}, f32[4,576,2304]{2,1,0:T(8,128)}) fusion(pred[576,2304]{1,0:T(8,128)(4,1)S(1)} %broadcast_compare_fusion.4, bf16[2304,4,128]{2,0,1:T(8,128)(2,1)S(1)} %get-tuple-element.352, bf16[1,576,4,128]{3,2,1,0:T(4,128)(2,1)S(1)} %constant_dynamic-slice_fusion.4), kind=kOutput, calls=%fused_computation.4.clone.1 | convolution fusion | flops 1374877440 | bytes 25519104 | tf_op jit(solution)/shard_map/while/body/eval_jaxpr/qhd,khd->hqk/dot_general | solution.py:29
  467.8 10.6 %fusion.69 = f32[4,576]{1,0:T(4,128)S(1)} fusion(f32[4,576,2304]{2,1,0:T(8,128)} %get-tuple-element.297, f32[4,576]{1,0:T(4,128)S(1)} %get-tuple-element.298, pred[576,2304]{1,0:T(8,128)(4,1)S(1)} %broadcast_compare_fusion.4), kind=kLoop, calls=%fused_computation.5.clone.1 | loop fusion | flops 21231360 | bytes 22579200 | tf_op jit(solution)/shard_map/while/body/eval_jaxpr/reduce_sum | solution.py:36
  478.4 10.5 %fusion.70 = bf16[4,576,4,128]{3,1,0,2:T(8,128)(2,1)} fusion(bf16[4,576,4,128]{3,1,0,2:T(8,128)(2,1)} %get-tuple-element.341, s32[]{:T(128)} %get-tuple-element.340, bf16[2304,4,128]{2,0,1:T(8,128)(2,1)S(1)} %copy-done.3, f32[4,576,2304]{2,1,0:T(8,128)} %get-tuple-element.297, f32[4,576]{1,0:T(4,128)S(1)} %get-tuple-element.298, ...), kind=kOutput, calls=%fused_computation.13.clone.1 | convolution fusion | flops 1380777984 | bytes 25528832 | tf_op jit(solution)/shard_map/while/body/eval_jaxpr/hqk,khd->qhd/dot_general | solution.py:37
  489.9 1.3 constant_dynamic-slice_fusion.4
  491.2 9.5 %fusion.68 = (f32[4,576]{1,0:T(4,128)S(1)}, f32[4,576,2304]{2,1,0:T(8,128)}) fusion(pred[576,2304]{1,0:T(8,128)(4,1)S(1)} %broadcast_compare_fusion.4, bf16[2304,4,128]{2,0,1:T(8,128)(2,1)S(1)} %get-tuple-element.352, bf16[1,576,4,128]{3,2,1,0:T(4,128)(2,1)S(1)} %constant_dynamic-slice_fusion.4), kind=kOutput, calls=%fused_computation.4.clone.1 | convolution fusion | flops 1374877440 | bytes 25519104 | tf_op jit(solution)/shard_map/while/body/eval_jaxpr/qhd,khd->hqk/dot_general | solution.py:29
  500.7 10.6 %fusion.69 = f32[4,576]{1,0:T(4,128)S(1)} fusion(f32[4,576,2304]{2,1,0:T(8,128)} %get-tuple-element.297, f32[4,576]{1,0:T(4,128)S(1)} %get-tuple-element.298, pred[576,2304]{1,0:T(8,128)(4,1)S(1)} %broadcast_compare_fusion.4), kind=kLoop, calls=%fused_computation.5.clone.1 | loop fusion | flops 21231360 | bytes 22579200 | tf_op jit(solution)/shard_map/while/body/eval_jaxpr/reduce_sum | solution.py:36
  511.4 10.5 %fusion.70 = bf16[4,576,4,128]{3,1,0,2:T(8,128)(2,1)} fusion(bf16[4,576,4,128]{3,1,0,2:T(8,128)(2,1)} %get-tuple-element.341, s32[]{:T(128)} %get-tuple-element.340, bf16[2304,4,128]{2,0,1:T(8,128)(2,1)S(1)} %copy-done.3, f32[4,576,2304]{2,1,0:T(8,128)} %get-tuple-element.297, f32[4,576]{1,0:T(4,128)S(1)} %get-tuple-element.298, ...), kind=kOutput, calls=%fused_computation.13.clone.1 | convolution fusion | flops 1380777984 | bytes 25528832 | tf_op jit(solution)/shard_map/while/body/eval_jaxpr/hqk,khd->qhd/dot_general | solution.py:37
  521.8 2.1 copy.32
  524.2 1.8 copy.33
  526.0 1.9 broadcast.86.clone2
  527.8 134.5 %while.23 = (s32[]{:T(128)}, bf16[4,576,4,128]{3,1,0,2:T(8,128)(2,1)}, s32[4,576]{1,0:T(4,128)}, bf16[4,576,4,128]{3,2,1,0:T(4,128)(2,1)}, bf16[2304,4,128]{2,0,...) while((s32[]{:T(128)}, bf16[4,576,4,128]{3,1,0,2:T(8,128)(2,1)}, ...), condition=%wide.region_7.8_spmd.clone, body=%wide.region_4.7_spmd.clone.sunk | while | flops 2778213888 | bytes 85615160 | solution.py:44
  529.5 1.3 constant_dynamic-slice_fusion.5
  530.8 9.5 %fusion.74 = (f32[4,576]{1,0:T(4,128)S(1)}, f32[4,576,2304]{2,1,0:T(8,128)}) fusion(pred[576,2304]{1,0:T(8,128)(4,1)S(1)} %broadcast_compare_fusion.5, bf16[2304,4,128]{2,0,1:T(8,128)(2,1)S(1)} %get-tuple-element.328, bf16[1,576,4,128]{3,2,1,0:T(4,128)(2,1)S(1)} %constant_dynamic-slice_fusion.5), kind=kOutput, calls=%fused_computation.22.clone.1 | convolution fusion | flops 1374877440 | bytes 25519104 | tf_op jit(solution)/shard_map/while/body/eval_jaxpr/qhd,khd->hqk/dot_general | solution.py:29
  540.4 10.6 %fusion.75 = f32[4,576]{1,0:T(4,128)S(1)} fusion(f32[4,576,2304]{2,1,0:T(8,128)} %get-tuple-element.306, f32[4,576]{1,0:T(4,128)S(1)} %get-tuple-element.307, pred[576,2304]{1,0:T(8,128)(4,1)S(1)} %broadcast_compare_fusion.5), kind=kLoop, calls=%fused_computation.23.clone.1 | loop fusion | flops 21231360 | bytes 22579200 | tf_op jit(solution)/shard_map/while/body/eval_jaxpr/reduce_sum | solution.py:36
  551.0 10.4 %fusion.76 = bf16[4,576,4,128]{3,1,0,2:T(8,128)(2,1)} fusion(bf16[4,576,4,128]{3,1,0,2:T(8,128)(2,1)} %get-tuple-element.317, s32[]{:T(128)} %get-tuple-element.316, bf16[2304,4,128]{2,0,1:T(8,128)(2,1)S(1)} %copy-done.2, f32[4,576,2304]{2,1,0:T(8,128)} %get-tuple-element.306, f32[4,576]{1,0:T(4,128)S(1)} %get-tuple-element.307, ...), kind=kOutput, calls=%fused_computation.31.clone.1 | convolution fusion | flops 1380777984 | bytes 25528832 | tf_op jit(solution)/shard_map/while/body/eval_jaxpr/hqk,khd->qhd/dot_general | solution.py:37
  563.2 1.3 constant_dynamic-slice_fusion.5
  564.4 9.5 %fusion.74 = (f32[4,576]{1,0:T(4,128)S(1)}, f32[4,576,2304]{2,1,0:T(8,128)}) fusion(pred[576,2304]{1,0:T(8,128)(4,1)S(1)} %broadcast_compare_fusion.5, bf16[2304,4,128]{2,0,1:T(8,128)(2,1)S(1)} %get-tuple-element.328, bf16[1,576,4,128]{3,2,1,0:T(4,128)(2,1)S(1)} %constant_dynamic-slice_fusion.5), kind=kOutput, calls=%fused_computation.22.clone.1 | convolution fusion | flops 1374877440 | bytes 25519104 | tf_op jit(solution)/shard_map/while/body/eval_jaxpr/qhd,khd->hqk/dot_general | solution.py:29
  574.0 10.6 %fusion.75 = f32[4,576]{1,0:T(4,128)S(1)} fusion(f32[4,576,2304]{2,1,0:T(8,128)} %get-tuple-element.306, f32[4,576]{1,0:T(4,128)S(1)} %get-tuple-element.307, pred[576,2304]{1,0:T(8,128)(4,1)S(1)} %broadcast_compare_fusion.5), kind=kLoop, calls=%fused_computation.23.clone.1 | loop fusion | flops 21231360 | bytes 22579200 | tf_op jit(solution)/shard_map/while/body/eval_jaxpr/reduce_sum | solution.py:36
  584.6 10.4 %fusion.76 = bf16[4,576,4,128]{3,1,0,2:T(8,128)(2,1)} fusion(bf16[4,576,4,128]{3,1,0,2:T(8,128)(2,1)} %get-tuple-element.317, s32[]{:T(128)} %get-tuple-element.316, bf16[2304,4,128]{2,0,1:T(8,128)(2,1)S(1)} %copy-done.2, f32[4,576,2304]{2,1,0:T(8,128)} %get-tuple-element.306, f32[4,576]{1,0:T(4,128)S(1)} %get-tuple-element.307, ...), kind=kOutput, calls=%fused_computation.31.clone.1 | convolution fusion | flops 1380777984 | bytes 25528832 | tf_op jit(solution)/shard_map/while/body/eval_jaxpr/hqk,khd->qhd/dot_general | solution.py:37
  596.8 1.3 constant_dynamic-slice_fusion.5
  598.0 9.5 %fusion.74 = (f32[4,576]{1,0:T(4,128)S(1)}, f32[4,576,2304]{2,1,0:T(8,128)}) fusion(pred[576,2304]{1,0:T(8,128)(4,1)S(1)} %broadcast_compare_fusion.5, bf16[2304,4,128]{2,0,1:T(8,128)(2,1)S(1)} %get-tuple-element.328, bf16[1,576,4,128]{3,2,1,0:T(4,128)(2,1)S(1)} %constant_dynamic-slice_fusion.5), kind=kOutput, calls=%fused_computation.22.clone.1 | convolution fusion | flops 1374877440 | bytes 25519104 | tf_op jit(solution)/shard_map/while/body/eval_jaxpr/qhd,khd->hqk/dot_general | solution.py:29
  607.6 10.6 %fusion.75 = f32[4,576]{1,0:T(4,128)S(1)} fusion(f32[4,576,2304]{2,1,0:T(8,128)} %get-tuple-element.306, f32[4,576]{1,0:T(4,128)S(1)} %get-tuple-element.307, pred[576,2304]{1,0:T(8,128)(4,1)S(1)} %broadcast_compare_fusion.5), kind=kLoop, calls=%fused_computation.23.clone.1 | loop fusion | flops 21231360 | bytes 22579200 | tf_op jit(solution)/shard_map/while/body/eval_jaxpr/reduce_sum | solution.py:36
  618.3 10.4 %fusion.76 = bf16[4,576,4,128]{3,1,0,2:T(8,128)(2,1)} fusion(bf16[4,576,4,128]{3,1,0,2:T(8,128)(2,1)} %get-tuple-element.317, s32[]{:T(128)} %get-tuple-element.316, bf16[2304,4,128]{2,0,1:T(8,128)(2,1)S(1)} %copy-done.2, f32[4,576,2304]{2,1,0:T(8,128)} %get-tuple-element.306, f32[4,576]{1,0:T(4,128)S(1)} %get-tuple-element.307, ...), kind=kOutput, calls=%fused_computation.31.clone.1 | convolution fusion | flops 1380777984 | bytes 25528832 | tf_op jit(solution)/shard_map/while/body/eval_jaxpr/hqk,khd->qhd/dot_general | solution.py:37
  630.4 1.3 constant_dynamic-slice_fusion.5
  631.7 9.5 %fusion.74 = (f32[4,576]{1,0:T(4,128)S(1)}, f32[4,576,2304]{2,1,0:T(8,128)}) fusion(pred[576,2304]{1,0:T(8,128)(4,1)S(1)} %broadcast_compare_fusion.5, bf16[2304,4,128]{2,0,1:T(8,128)(2,1)S(1)} %get-tuple-element.328, bf16[1,576,4,128]{3,2,1,0:T(4,128)(2,1)S(1)} %constant_dynamic-slice_fusion.5), kind=kOutput, calls=%fused_computation.22.clone.1 | convolution fusion | flops 1374877440 | bytes 25519104 | tf_op jit(solution)/shard_map/while/body/eval_jaxpr/qhd,khd->hqk/dot_general | solution.py:29
  641.2 10.6 %fusion.75 = f32[4,576]{1,0:T(4,128)S(1)} fusion(f32[4,576,2304]{2,1,0:T(8,128)} %get-tuple-element.306, f32[4,576]{1,0:T(4,128)S(1)} %get-tuple-element.307, pred[576,2304]{1,0:T(8,128)(4,1)S(1)} %broadcast_compare_fusion.5), kind=kLoop, calls=%fused_computation.23.clone.1 | loop fusion | flops 21231360 | bytes 22579200 | tf_op jit(solution)/shard_map/while/body/eval_jaxpr/reduce_sum | solution.py:36
  651.9 10.4 %fusion.76 = bf16[4,576,4,128]{3,1,0,2:T(8,128)(2,1)} fusion(bf16[4,576,4,128]{3,1,0,2:T(8,128)(2,1)} %get-tuple-element.317, s32[]{:T(128)} %get-tuple-element.316, bf16[2304,4,128]{2,0,1:T(8,128)(2,1)S(1)} %copy-done.2, f32[4,576,2304]{2,1,0:T(8,128)} %get-tuple-element.306, f32[4,576]{1,0:T(4,128)S(1)} %get-tuple-element.307, ...), kind=kOutput, calls=%fused_computation.31.clone.1 | convolution fusion | flops 1380777984 | bytes 25528832 | tf_op jit(solution)/shard_map/while/body/eval_jaxpr/hqk,khd->qhd/dot_general | solution.py:37
  662.3 2.8 pad_maximum_fusion.3
  665.1 12.0 %copy.35 = bf16[2,2304,4,128]{3,2,1,0:T(4,128)(2,1)} copy(bf16[2,2304,4,128]{3,1,2,0:T(8,128)(2,1)S(1)} %pad_maximum_fusion.3) | data formatting | bytes 9437184 | tf_op jit(solution)/shard_map/stack | solution.py:67
  677.1 8.0 reshape.108
  685.2 1.5 slice.102
  687.3 2.5 collective-permute-done.2
  690.1 56.5 %all_to_all.24 = bf16[96,48,512]{2,1,0:T(8,128)(2,1)S(1)} all-to-all(bf16[96,48,512]{2,1,0:T(8,128)(2,1)S(1)} %pad_maximum_fusion.4), channel_id=1, replica_groups=mesh['win'=16,'head'=2] {'head'}, dimensions={0} | all-to-all | bytes 9437184 | tf_op jit(solution)/shard_map/all_to_all | solution.py:90
  748.2 55.7 %collective-permute-done.3 = bf16[48,24,1024]{2,1,0:T(8,128)(2,1)S(1)} collective-permute-done((bf16[48,24,1024]{2,1,0:T(8,128)(2,1)S(1)}, bf16[48,24,1024]{2,1,0:T(8,128)(2,1)S(1)}, u32[]{:S(2)}, u32[]{:S(2)}) %collective-permute-start.3) | collective-permute-done | bytes 2359328 | tf_op jit(solution)/shard_map/ppermute | solution.py:12
  803.9 2.7 maximum_bitcast_fusion
  (67 shorter events, 15.3 us)
Async XLA Ops:
  6.1 157.7 %collective-permute-start = (bf16[3,48,24,1024]{3,2,1,0:T(8,128)(2,1)S(1)}, bf16[3,48,24,1024]{3,2,1,0:T(8,128)(2,1)S(1)}, u32[]{:S(2)}, u32[]{:S(2)}) collective-permute-start(bf16[3,48,24,1024]{3,2,1,0:T(8,128)(2,1)S(1)} %get-tuple-element.207), channel_id=1, source_target_pairs={{0,28},{2,30},{4,0},{6,2},{8,4},{10,6},{12,8},{14,10},{16,12},{18,... | collective-permute-start | bytes 21233672 | tf_op jit(solution)/shard_map/ppermute | solution.py:12
  326.8 5.1 copy-start
  333.9 12.4 %collective-permute-start.1 = (bf16[3,24,48,512]{3,2,1,0:T(8,128)(2,1)}, bf16[3,24,48,512]{3,2,1,0:T(8,128)(2,1)S(1)}, u32[]{:S(2)}, u32[]{:S(2)}) collective-permute-start(bf16[3,24,48,512]{3,2,1,0:T(8,128)(2,1)} %slice.95), channel_id=1, source_target_pairs={{0,2},{2,0},{4,6},{6,4},{8,10},{10,8},{12,14},{14,12},{16,18},{18,... | collective-permute-start | bytes 10616840 | tf_op jit(solution)/shard_map/ppermute | solution.py:18
  401.9 10.7 %copy-start.3 = (bf16[2304,4,128]{2,0,1:T(8,128)(2,1)S(1)}, bf16[2304,4,128]{2,0,1:T(8,128)(2,1)}, u32[]{:S(2)}) copy-start(bf16[2304,4,128]{2,0,1:T(8,128)(2,1)} %get-tuple-element.353) | copy-start | bytes 7077892 | tf_op jit(solution)/shard_map/while
  434.8 10.7 %copy-start.3 = (bf16[2304,4,128]{2,0,1:T(8,128)(2,1)S(1)}, bf16[2304,4,128]{2,0,1:T(8,128)(2,1)}, u32[]{:S(2)}) copy-start(bf16[2304,4,128]{2,0,1:T(8,128)(2,1)} %get-tuple-element.353) | copy-start | bytes 7077892 | tf_op jit(solution)/shard_map/while
  467.8 10.7 %copy-start.3 = (bf16[2304,4,128]{2,0,1:T(8,128)(2,1)S(1)}, bf16[2304,4,128]{2,0,1:T(8,128)(2,1)}, u32[]{:S(2)}) copy-start(bf16[2304,4,128]{2,0,1:T(8,128)(2,1)} %get-tuple-element.353) | copy-start | bytes 7077892 | tf_op jit(solution)/shard_map/while
  500.7 10.7 %copy-start.3 = (bf16[2304,4,128]{2,0,1:T(8,128)(2,1)S(1)}, bf16[2304,4,128]{2,0,1:T(8,128)(2,1)}, u32[]{:S(2)}) copy-start(bf16[2304,4,128]{2,0,1:T(8,128)(2,1)} %get-tuple-element.353) | copy-start | bytes 7077892 | tf_op jit(solution)/shard_map/while
  521.8 2.4 copy-start.1
  521.8 6.0 copy-start.4
  540.4 10.7 %copy-start.2 = (bf16[2304,4,128]{2,0,1:T(8,128)(2,1)S(1)}, bf16[2304,4,128]{2,0,1:T(8,128)(2,1)}, u32[]{:S(2)}) copy-start(bf16[2304,4,128]{2,0,1:T(8,128)(2,1)} %get-tuple-element.329) | copy-start | bytes 7077892 | tf_op jit(solution)/shard_map/while
  574.0 10.7 %copy-start.2 = (bf16[2304,4,128]{2,0,1:T(8,128)(2,1)S(1)}, bf16[2304,4,128]{2,0,1:T(8,128)(2,1)}, u32[]{:S(2)}) copy-start(bf16[2304,4,128]{2,0,1:T(8,128)(2,1)} %get-tuple-element.329) | copy-start | bytes 7077892 | tf_op jit(solution)/shard_map/while
  607.6 10.7 %copy-start.2 = (bf16[2304,4,128]{2,0,1:T(8,128)(2,1)S(1)}, bf16[2304,4,128]{2,0,1:T(8,128)(2,1)}, u32[]{:S(2)}) copy-start(bf16[2304,4,128]{2,0,1:T(8,128)(2,1)} %get-tuple-element.329) | copy-start | bytes 7077892 | tf_op jit(solution)/shard_map/while
  641.2 10.7 %copy-start.2 = (bf16[2304,4,128]{2,0,1:T(8,128)(2,1)S(1)}, bf16[2304,4,128]{2,0,1:T(8,128)(2,1)}, u32[]{:S(2)}) copy-start(bf16[2304,4,128]{2,0,1:T(8,128)(2,1)} %get-tuple-element.329) | copy-start | bytes 7077892 | tf_op jit(solution)/shard_map/while
  685.2 4.5 slice-start
  686.7 3.0 collective-permute-start.2
  747.8 56.1 %collective-permute-start.3 = (bf16[48,24,1024]{2,1,0:T(8,128)(2,1)S(1)}, bf16[48,24,1024]{2,1,0:T(8,128)(2,1)S(1)}, u32[]{:S(2)}, u32[]{:S(2)}) collective-permute-start(bf16[48,24,1024]{2,1,0:T(8,128)(2,1)S(1)} %get-tuple-element.208), channel_id=1, source_target_pairs={{0,4},{2,6},{4,8},{6,10},{8,12},{10,14},{12,16},{14,18},{16,20},{1... | collective-permute-start | bytes 7077896 | tf_op jit(solution)/shard_map/ppermute | solution.py:12
